TPU v7x, 32 devices: a whole 2x2x4 slice. The times are simulated.
32 devices in a mesh: bank: 4 (over z), zero: 8 (over y, x, core).
Axes of the slice: x: 2, y: 2, z: 4, core: 2. Of those that a mesh axis runs over, the one named last changes fastest.
Arguments:
- master_gate: float32 [64, 2048, 1024], P('bank', 'zero'), may hold values from -0.1875 to 0.1875
- second_gate: bfloat16 [64, 2048, 1024], P('bank', 'zero'), may hold values from -0.0625 to 0.0625
- master_up: float32 [64, 2048, 1024], P('bank', 'zero'), may hold values from -0.1875 to 0.1875
- second_up: bfloat16 [64, 2048, 1024], P('bank', 'zero'), may hold values from -0.0625 to 0.0625
- master_down: float32 [64, 1024, 2048], P('bank', None, 'zero'), may hold values from -0.25 to 0.25
- second_down: bfloat16 [64, 1024, 2048], P('bank', None, 'zero'), may hold values from -0.09375 to 0.09375
- router_weight: float32 [2048, 64], P('zero', 'bank'), may hold values from -0.125 to 0.125
- router_gain: float32 [2048], P('zero'), may hold values from 0.25 to 1.75
Outputs:
- final_gate: bfloat16 [64, 2048, 1024], P('bank', None, 'zero')
- final_up: bfloat16 [64, 2048, 1024], P('bank', None, 'zero')
- final_down: bfloat16 [64, 1024, 2048], P('bank', 'zero')
- scale_gate: float32 [64, 1024], P('bank', 'zero')
- scale_up: float32 [64, 1024], P('bank', 'zero')
- scale_down: float32 [64, 1024], P('bank', 'zero')
- serve_router: bfloat16 [2048, 64], replicated
All inputs are finite; a program needn't handle non-finite values. Where the computation divides by a largest or mean magnitude, that divisor is 1e-20 or more.
Results may differ from a plain program's by a relative error of at most 0.001.
Values may be sent and summed in bfloat16 or wider, within the bound.
No kernel may reach another device: no remote copies, remote signals or barrier semaphores. Data moves between devices by JAX's collectives and lax.ppermute only.
A program may use at most 192 MiB of HBM per device.

v0:
```python
import jax
import jax.numpy as jnp
from jax import lax
from jax.sharding import PartitionSpec as P

D_MODEL = 2048


def on_device(
    master_gate,
    second_gate,
    master_up,
    second_up,
    master_down,
    second_down,
    router_weight,
    router_gain,
):
    merged_gate = master_gate + second_gate.astype(jnp.float32)
    merged_up = master_up + second_up.astype(jnp.float32)
    merged_down = master_down + second_down.astype(jnp.float32)
    total_gate, total_up, total_down = lax.psum(
        (
            jnp.sum(jnp.abs(merged_gate), axis=1),
            jnp.sum(jnp.abs(merged_up), axis=1),
            jnp.sum(jnp.abs(merged_down), axis=2),
        ),
        "zero",
    )
    scale_gate = total_gate / D_MODEL
    scale_up = total_up / D_MODEL
    scale_down = total_down / D_MODEL
    narrow_gate, narrow_up, narrow_down = (
        (merged_gate / jnp.expand_dims(scale_gate, 1)).astype(jnp.bfloat16),
        (merged_up / jnp.expand_dims(scale_up, 1)).astype(jnp.bfloat16),
        (merged_down / jnp.expand_dims(scale_down, 2)).astype(jnp.bfloat16),
    )
    final_gate, final_up = (
        lax.all_to_all(narrow_gate, "zero", split_axis=2, concat_axis=1, tiled=True),
        lax.all_to_all(narrow_up, "zero", split_axis=2, concat_axis=1, tiled=True),
    )
    final_down = lax.all_to_all(narrow_down, "zero", split_axis=1, concat_axis=2, tiled=True)
    scale_gate = lax.dynamic_slice_in_dim(
        scale_gate, lax.axis_index("zero") * final_gate.shape[2], final_gate.shape[2], axis=1
    )
    scale_up = lax.dynamic_slice_in_dim(
        scale_up, lax.axis_index("zero") * final_up.shape[2], final_up.shape[2], axis=1
    )
    scale_down = lax.dynamic_slice_in_dim(
        scale_down, lax.axis_index("zero") * final_down.shape[1], final_down.shape[1], axis=1
    )
    part_router = (router_weight * router_gain[:, None]).astype(jnp.bfloat16)
    row_router = lax.all_gather(part_router, "zero", axis=0, tiled=True)
    serve_router = lax.all_gather(row_router, "bank", axis=1, tiled=True)
    return (final_gate, final_up, final_down, scale_gate, scale_up, scale_down, serve_router)


def solution(mesh):
    return jax.shard_map(
        on_device,
        mesh=mesh,
        in_specs=(
            P("bank", "zero", None),
            P("bank", "zero", None),
            P("bank", "zero", None),
            P("bank", "zero", None),
            P("bank", None, "zero"),
            P("bank", None, "zero"),
            P("zero", "bank"),
            P("zero"),
        ),
        out_specs=(
            P("bank", None, "zero"),
            P("bank", None, "zero"),
            P("bank", "zero", None),
            P("bank", "zero"),
            P("bank", "zero"),
            P("bank", "zero"),
            P(),
        ),
        check_vma=False,
    )
```

profile of v0, /device:TPU:0, one launch (start us, length us, event | category | flops | bytes accessed | tf_op | source)
XLA Modules:
  0.0 554.7 jit_solution(10408405090956699153)
XLA Ops:
  7.2 17.6 %copy.31 = f32[16,256,1024]{1,0,2:T(8,128)} copy(f32[16,256,1024]{2,1,0:T(8,128)} %param.8) | data formatting | bytes 33554432 | tf_op args[0]
  24.8 17.6 %copy.34 = f32[16,256,1024]{1,0,2:T(8,128)} copy(f32[16,256,1024]{2,1,0:T(8,128)} %param.10) | data formatting | bytes 33554432 | tf_op args[2]
  42.4 12.5 %copy.30 = bf16[16,256,1024]{1,0,2:T(8,128)(2,1)} copy(bf16[16,256,1024]{2,1,0:T(8,128)(2,1)} %param.9) | data formatting | bytes 16777216 | tf_op args[1]
  54.9 12.5 %copy.33 = bf16[16,256,1024]{1,0,2:T(8,128)(2,1)} copy(bf16[16,256,1024]{2,1,0:T(8,128)(2,1)} %param.11) | data formatting | bytes 16777216 | tf_op args[3]
  67.4 25.3 %abs_reduce_fusion = f32[16,1024]{0,1:T(8,128)} fusion(f32[16,1024,256]{2,1,0:T(8,128)} %param.12, bf16[16,1024,256]{2,1,0:T(8,128)(2,1)} %param.13), kind=kLoop, calls=%fused_computation.2 | loop fusion | flops 16760832 | bytes 25231360 | tf_op jit(solution)/shard_map/reduce_sum | solution.py:26
  92.7 13.2 %abs_reduce_fusion.1 = (f32[16,1024]{0,1:T(8,128)}, f32[16,1024]{0,1:T(8,128)}) fusion(f32[16,256,1024]{1,0,2:T(8,128)} %copy.34, bf16[16,256,1024]{1,0,2:T(8,128)(2,1)S(1)} %copy-done.1, f32[16,256,1024]{1,0,2:T(8,128)} %copy.31, bf16[16,256,1024]{1,0,2:T(8,128)(2,1)S(1)} %copy-done), kind=kLoop, calls=%fused_computation.4 | loop fusion | flops 33521664 | bytes 50462720 | tf_op jit(solution)/shard_map/reduce_sum | solution.py:25
  105.9 62.0 %all-reduce.3.cloned.1.call-done = (f32[16,1024]{0,1:T(8,128)}, f32[16,1024]{0,1:T(8,128)}, f32[16,1024]{0,1:T(8,128)}) async-done(((f32[16,1024]{0,1:T(8,128)}, f32[16,1024]{0,1:T(8,128)}, f32[16,1024]{0,1:T(8,128)}), (f32[16,1024]{0,1:T(8,128)}, f32[16,1024]{0,1:T(8,128)}, f32[16,1024]{0,1:T(8,128)})) %all-reduce.3.cloned.1.call-update) | async-done | bytes 196624 | tf_op jit(solution)/shard_map/psum | solution.py:22
  167.9 1.1 broadcast_multiply_fusion.1
  169.0 12.0 %divide_convert_fusion.1 = bf16[16,256,1024]{1,0,2:T(8,128)(2,1)} fusion(f32[16,256,1024]{1,0,2:T(8,128)} %copy.34, bf16[16,256,1024]{1,0,2:T(8,128)(2,1)} %copy.33, f32[16,1024]{0,1:T(8,128)S(1)} %broadcast_multiply_fusion.1), kind=kLoop, calls=%fused_computation.3 | loop fusion | flops 16777216 | bytes 33619968 | tf_op jit(solution)/shard_map/convert_element_type | solution.py:35
  180.9 5.1 all-to-all-start.1
  186.1 12.0 %divide_convert_fusion.2 = bf16[16,256,1024]{1,0,2:T(8,128)(2,1)} fusion(f32[16,256,1024]{1,0,2:T(8,128)} %copy.31, bf16[16,256,1024]{1,0,2:T(8,128)(2,1)} %copy.30, f32[16,1024]{0,1:T(8,128)S(1)} %broadcast_multiply_fusion.2), kind=kLoop, calls=%fused_computation.6 | loop fusion | flops 16777216 | bytes 33619968 | tf_op jit(solution)/shard_map/convert_element_type | solution.py:34
  198.1 82.0 %all-to-all-done.1 = bf16[16,256,1024]{1,0,2:T(8,128)(2,1)} async-done(((bf16[16,256,1024]{1,0,2:T(8,128)(2,1)}), bf16[16,256,1024]{1,0,2:T(8,128)(2,1)}, u32[]{:S(2)}, u32[]{:S(2)}) %all-to-all-start.1) | async-done | bytes 8388640 | tf_op jit(solution)/shard_map/all_to_all | solution.py:40
  280.1 5.1 all-to-all-start
  285.3 23.8 %divide_convert_fusion = bf16[16,1024,256]{2,0,1:T(8,128)(2,1)} fusion(f32[16,1024,256]{2,1,0:T(8,128)} %param.12, f32[16,1024]{0,1:T(8,128)S(1)} %broadcast_multiply_fusion, bf16[16,1024,256]{2,1,0:T(8,128)(2,1)} %param.13), kind=kLoop, calls=%fused_computation.1 | loop fusion | flops 16777216 | bytes 33619968 | tf_op jit(solution)/shard_map/convert_element_type | solution.py:36
  309.0 70.0 %all-to-all-done = bf16[16,256,1024]{1,0,2:T(8,128)(2,1)} async-done(((bf16[16,256,1024]{1,0,2:T(8,128)(2,1)}), bf16[16,256,1024]{1,0,2:T(8,128)(2,1)}, u32[]{:S(2)}, u32[]{:S(2)}) %all-to-all-start) | async-done | bytes 8388640 | tf_op jit(solution)/shard_map/all_to_all | solution.py:39
  379.1 5.0 all-to-all-start.2
  384.1 97.2 %all_gather.6 = bf16[2048,16]{0,1:T(8,128)(2,1)S(1)} all-gather(bf16[256,16]{0,1:T(8,128)(2,1)S(1)} %multiply_convert_fusion), channel_id=1, replica_groups=mesh['bank'=4,'zero'=8] {'zero'}, dimensions={0}, use_global_device_ids=true | all-gather | bytes 73728 | tf_op jit(solution)/shard_map/all_gather | solution.py:53
  481.3 14.4 %all_gather.7 = bf16[2048,64]{0,1:T(8,128)(2,1)S(1)} all-gather(bf16[2048,16]{0,1:T(8,128)(2,1)S(1)} %all_gather.6), channel_id=1, replica_groups=mesh['bank'=4,'zero'=8] {'bank'}, dimensions={1}, use_global_device_ids=true | all-gather | bytes 327680 | tf_op jit(solution)/shard_map/all_gather | solution.py:54
  495.7 0.7 copy.39
  497.8 12.3 %copy.35 = bf16[16,8,256,128]{3,2,1,0:T(8,128)(2,1)} copy(bf16[16,8,256,128]{2,0,3,1:T(8,128)(2,1)} %bitcast.4) | data formatting | bytes 16777216 | tf_op jit(solution)/shard_map/all_to_all | solution.py:40
  510.0 12.3 %copy.32 = bf16[16,8,256,128]{3,2,1,0:T(8,128)(2,1)} copy(bf16[16,8,256,128]{2,0,3,1:T(8,128)(2,1)} %bitcast.1) | data formatting | bytes 16777216 | tf_op jit(solution)/shard_map/all_to_all | solution.py:39
  522.3 11.4 %copy.38 = bf16[16,128,8,256]{3,2,1,0:T(8,128)(2,1)} copy(bf16[16,128,8,256]{3,0,1,2:T(8,128)(2,1)} %bitcast.7) | data formatting | bytes 16777216 | tf_op jit(solution)/shard_map/all_to_all | solution.py:42
  533.7 13.4 %all_to_all.50 = bf16[16,128,2048]{2,1,0:T(8,128)(2,1)} reshape(bf16[16,128,8,256]{3,2,1,0:T(8,128)(2,1)} %copy.38) | data formatting | bytes 16777216 | tf_op jit(solution)/shard_map/all_to_all | solution.py:42
  547.1 0.7 copy.53
  (23 shorter events, 1.5 us)
Async XLA Ops:
  7.2 160.7 %all-reduce.3.cloned.1.call-start = ((), (), s32[]{:S(2)}) async-start(), calls=%async_computation.3 | async-start | bytes 3145728 | tf_op jit(solution)/shard_map/psum | solution.py:22
  67.4 25.3 %copy-start = (bf16[16,256,1024]{1,0,2:T(8,128)(2,1)S(1)}, bf16[16,256,1024]{1,0,2:T(8,128)(2,1)}, u32[]{:S(2)}) copy-start(bf16[16,256,1024]{1,0,2:T(8,128)(2,1)} %copy.30) | copy-start | bytes 25165828
  67.4 25.3 %copy-start.1 = (bf16[16,256,1024]{1,0,2:T(8,128)(2,1)S(1)}, bf16[16,256,1024]{1,0,2:T(8,128)(2,1)}, u32[]{:S(2)}) copy-start(bf16[16,256,1024]{1,0,2:T(8,128)(2,1)} %copy.33) | copy-start | bytes 25165828
  180.9 5.1 copy-start.3
  180.9 99.1 %all-to-all-start.1 = ((bf16[16,256,1024]{1,0,2:T(8,128)(2,1)}), bf16[16,256,1024]{1,0,2:T(8,128)(2,1)}, u32[]{:S(2)}, u32[]{:S(2)}) async-start(bf16[16,256,1024]{1,0,2:T(8,128)(2,1)} %divide_convert_fusion.1), calls=%async_computation.1 | async-start | bytes 16777216 | tf_op jit(solution)/shard_map/all_to_all | solution.py:40
  198.1 87.1 %copy-start.2 = (f32[16,1024]{0,1:T(8,128)S(1)}, f32[16,1024]{0,1:T(8,128)}, u32[]{:S(2)}) copy-start(f32[16,1024]{0,1:T(8,128)} %get-tuple-element.16) | copy-start | bytes 196612
  280.1 99.0 %all-to-all-start = ((bf16[16,256,1024]{1,0,2:T(8,128)(2,1)}), bf16[16,256,1024]{1,0,2:T(8,128)(2,1)}, u32[]{:S(2)}, u32[]{:S(2)}) async-start(bf16[16,256,1024]{1,0,2:T(8,128)(2,1)} %divide_convert_fusion.2), calls=%async_computation | async-start | bytes 16777216 | tf_op jit(solution)/shard_map/all_to_all | solution.py:39
  309.0 75.1 %copy-start.4 = (f32[256,16]{0,1:T(8,128)S(1)}, f32[256,16]{0,1:T(8,128)}, u32[]{:S(2)}) copy-start(f32[256,16]{0,1:T(8,128)} %param.14) | copy-start | bytes 49156
  309.0 75.1 %copy-start.5 = (f32[256]{0:T(256)S(1)}, f32[256]{0:T(256)}, u32[]{:S(2)}) copy-start(f32[256]{0:T(256)} %param.15) | copy-start | bytes 3076
  379.1 143.3 %all-to-all-start.2 = ((bf16[16,1024,256]{2,0,1:T(8,128)(2,1)}), bf16[16,1024,256]{2,0,1:T(8,128)(2,1)}, u32[]{:S(2)}, u32[]{:S(2)}) async-start(bf16[16,1024,256]{2,0,1:T(8,128)(2,1)} %divide_convert_fusion), calls=%async_computation.2 | async-start | bytes 16777216 | tf_op jit(solution)/shard_map/all_to_all | solution.py:42
Sparse Core Ops, SparseCore 0:
  106.0 61.7 all-reduce.2
where the time goes:
time: 557 us; the launch traced here: 555 us
  waiting for transfers between devices  214 us (38%)
  local copies, waits for them, and re-layouts  112 us (20%)
  blocking collectives  112 us (20%)
  other arithmetic  87.4 us (16%)
  starting transfers between devices  15.3 us (3%)
  between operations  14.1 us (3%)
    all_gather x1, blocking collectives, on_device(): row_router = lax.all_gather(part_router, 'zero', axis=0, tiled=True)  97.2 us
    all_to_all x1, waiting for transfers between devices, on_device(): lax.all_to_all(narrow_up, 'zero', split_axis=2, concat_axis=1, tiled=True)  82 us
    all_to_all x1, waiting for transfers between devices, on_device(): lax.all_to_all(narrow_gate, 'zero', split_axis=2, concat_axis=1, tiled=True)  70 us
    unnamed x20, local copies, waits for them, and re-layouts  62.9 us
    psum x1, waiting for transfers between devices, on_device(): lax.psum((jnp.sum(jnp.abs(merged_gate), axis=1), jnp.sum(jnp.abs(merged_u...  62 us
    reduce_sum x1, other arithmetic, on_device(): jnp.sum(jnp.abs(merged_down), axis=2)  25.3 us
    all_to_all x2, local copies, waits for them, and re-layouts, on_device(): lax.all_to_all(narrow_down, 'zero', split_axis=1, concat_axis=2, tiled=True)  24.8 us
    convert_element_type x1, other arithmetic, on_device(): (merged_down / jnp.expand_dims(scale_down, 2)).astype(jnp.bfloat16)  23.8 us
  transfers between devices with their start and end apart: 4, of which 3 were waited for; matrix products, arithmetic and copies ran while one was open for 11% of the time, Pallas kernels for 0%

commit v1 on v0

--- a/solution.py
+++ b/solution.py
@@ -4,6 +4,13 @@
 from jax.sharding import PartitionSpec as P
 
 D_MODEL = 2048
+
+
+def trade_parts(array, axis, split, join):
+    size = lax.axis_size(axis)
+    blocks = jnp.stack(jnp.split(array, size, axis=split), axis=0)
+    blocks = lax.all_to_all(blocks, axis, split_axis=0, concat_axis=0)
+    return jnp.concatenate(blocks, axis=join)
 
 
 def on_device(
@@ -36,7 +43,7 @@
         (merged_down / jnp.expand_dims(scale_down, 2)).astype(jnp.bfloat16),
     )
     final_gate, final_up = (
-        lax.all_to_all(narrow_gate, "zero", split_axis=2, concat_axis=1, tiled=True),
+        trade_parts(narrow_gate, "zero", 2, 1),
         lax.all_to_all(narrow_up, "zero", split_axis=2, concat_axis=1, tiled=True),
     )
     final_down = lax.all_to_all(narrow_down, "zero", split_axis=1, concat_axis=2, tiled=True)

time: 557 us -> 522 us (0.937)
  local copies, waits for them, and re-layouts: 112 us -> 88.9 us
  waiting for transfers between devices: 214 us -> 202 us
    all_to_all x1, waiting for transfers between devices: 0.01 us -> 74.6 us  [on_device(): lax.all_to_all(narrow_down, 'zero', split_axis=1, concat_axis=2, tiled=True)]
    all_to_all x1, waiting for transfers between devices: 70 us -> 0.01 us  [trade_parts(): blocks = lax.all_to_all(blocks, axis, split_axis=0, concat_axis=0)]
    unnamed x20 -> x18, local copies, waits for them, and re-layouts: 62.9 us -> 39.5 us
    all_to_all x1 -> x0, local copies, waits for them, and re-layouts: 12.3 us -> none  [on_device(): lax.all_to_all(narrow_gate, 'zero', split_axis=2, concat_axis=1, tiled=True)]
    all_to_all x1, waiting for transfers between devices: 82 us -> 69.8 us  [on_device(): lax.all_to_all(narrow_up, 'zero', split_axis=2, concat_axis=1, tiled=True)]
    reduce_sum x0 -> x1, other arithmetic: none -> 9.81 us  [on_device(): jnp.sum(jnp.abs(merged_gate), axis=1)]
    reshape x0 -> x1, local copies, waits for them, and re-layouts: none -> 7.89 us  [trade_parts(): return jnp.concatenate(blocks, axis=join)]
  transfers between devices with their start and end apart: 4 -> 4, of which waited for: 3 -> 3; matrix products, arithmetic and copies ran while one was open for 11% -> 13% of each run, Pallas kernels for 0% -> 0%
where the time goes in v1:
time: 522 us; the launch traced here: 521 us
  waiting for transfers between devices  202 us (39%)
  blocking collectives  111 us (21%)
  other arithmetic  89.4 us (17%)
  local copies, waits for them, and re-layouts  88.9 us (17%)
  starting transfers between devices  15.2 us (3%)
  between operations  14.2 us (3%)
    all_gather x1, blocking collectives, on_device(): row_router = lax.all_gather(part_router, 'zero', axis=0, tiled=True)  97.2 us
    all_to_all x1, waiting for transfers between devices, on_device(): lax.all_to_all(narrow_down, 'zero', split_axis=1, concat_axis=2, tiled=True)  74.6 us
    all_to_all x1, waiting for transfers between devices, on_device(): lax.all_to_all(narrow_up, 'zero', split_axis=2, concat_axis=1, tiled=True)  69.8 us
    psum x1, waiting for transfers between devices, on_device(): lax.psum((jnp.sum(jnp.abs(merged_gate), axis=1), jnp.sum(jnp.abs(merged_u...  57.2 us
    unnamed x18, local copies, waits for them, and re-layouts  39.5 us
    all_to_all x2, local copies, waits for them, and re-layouts, on_device(): lax.all_to_all(narrow_down, 'zero', split_axis=1, concat_axis=2, tiled=True)  24.8 us
    reduce_sum x1, other arithmetic, on_device(): jnp.sum(jnp.abs(merged_down), axis=2)  24.4 us
    convert_element_type x1, other arithmetic, on_device(): (merged_down / jnp.expand_dims(scale_down, 2)).astype(jnp.bfloat16)  23.8 us
  transfers between devices with their start and end apart: 4, of which 3 were waited for; matrix products, arithmetic and copies ran while one was open for 13% of the time, Pallas kernels for 0%

profile of v1, /device:TPU:0, one launch (start us, length us, event | category | flops | bytes accessed | tf_op | source)
XLA Modules:
  0.0 520.8 jit_solution(9076550071227375813)
XLA Ops:
  7.2 24.4 %abs_reduce_fusion = f32[16,1024]{0,1:T(8,128)S(1)} fusion(f32[16,1024,256]{2,1,0:T(8,128)} %param.12, bf16[16,1024,256]{2,1,0:T(8,128)(2,1)} %param.13), kind=kLoop, calls=%fused_computation.2 | loop fusion | flops 16760832 | bytes 25231360 | tf_op jit(solution)/shard_map/reduce_sum | solution.py:33
  32.4 12.5 %copy.39 = bf16[16,256,1024]{1,0,2:T(8,128)(2,1)} copy(bf16[16,256,1024]{2,1,0:T(8,128)(2,1)} %param.11) | data formatting | bytes 16777216 | tf_op args[3]
  44.9 17.6 %copy.40 = f32[16,256,1024]{1,0,2:T(8,128)} copy(f32[16,256,1024]{2,1,0:T(8,128)} %param.10) | data formatting | bytes 33554432 | tf_op args[2]
  62.5 9.1 %abs_reduce_fusion.1 = f32[16,1024]{0,1:T(8,128)S(1)} fusion(f32[16,256,1024]{1,0,2:T(8,128)} %copy.40, bf16[16,256,1024]{1,0,2:T(8,128)(2,1)} %copy.39), kind=kLoop, calls=%fused_computation.4 | loop fusion | flops 16760832 | bytes 25231360 | tf_op jit(solution)/shard_map/reduce_sum | solution.py:32
  72.4 9.8 %abs_reduce_fusion.2 = f32[16,1024]{1,0:T(8,128)} fusion(f32[16,256,1024]{2,1,0:T(8,128)} %param.8, bf16[16,256,1024]{2,1,0:T(8,128)(2,1)} %param.9), kind=kLoop, calls=%fused_computation.7 | loop fusion | flops 16760832 | bytes 25231360 | tf_op jit(solution)/shard_map/reduce_sum | solution.py:31
  82.3 57.2 %all-reduce.3.cloned.1.call-done = (f32[16,1024]{1,0:T(8,128)}, f32[16,1024]{1,0:T(8,128)}, f32[16,1024]{1,0:T(8,128)}) async-done(((f32[16,1024]{1,0:T(8,128)}, f32[16,1024]{1,0:T(8,128)}, f32[16,1024]{1,0:T(8,128)}), (f32[16,1024]{1,0:T(8,128)}, f32[16,1024]{1,0:T(8,128)}, f32[16,1024]{1,0:T(8,128)})) %all-reduce.3.cloned.1.call-update) | async-done | bytes 196624 | tf_op jit(solution)/shard_map/psum | solution.py:29
  140.6 12.0 %divide_convert_fusion.1 = bf16[16,256,1024]{1,0,2:T(8,128)(2,1)} fusion(f32[16,256,1024]{1,0,2:T(8,128)} %copy.40, bf16[16,256,1024]{1,0,2:T(8,128)(2,1)} %copy.39, f32[16,1024]{0,1:T(8,128)S(1)} %copy.42), kind=kLoop, calls=%fused_computation.3 | loop fusion | flops 16777216 | bytes 33619968 | tf_op jit(solution)/shard_map/convert_element_type | solution.py:42
  152.5 5.3 %all-to-all-start.1 = ((bf16[16,256,1024]{1,0,2:T(8,128)(2,1)}), bf16[16,256,1024]{1,0,2:T(8,128)(2,1)}, u32[]{:S(2)}, u32[]{:S(2)}) async-start(bf16[16,256,1024]{1,0,2:T(8,128)(2,1)} %divide_convert_fusion.1), calls=%async_computation.1 | async-start | bytes 16777216 | tf_op jit(solution)/shard_map/all_to_all | solution.py:47
  158.1 23.8 %divide_convert_fusion = bf16[16,1024,256]{2,0,1:T(8,128)(2,1)} fusion(f32[16,1024,256]{2,1,0:T(8,128)} %param.12, f32[16,1024]{0,1:T(8,128)S(1)} %copy.47, bf16[16,1024,256]{2,1,0:T(8,128)(2,1)} %param.13), kind=kLoop, calls=%fused_computation.1 | loop fusion | flops 16777216 | bytes 33619968 | tf_op jit(solution)/shard_map/convert_element_type | solution.py:43
  181.9 69.8 %all-to-all-done.1 = bf16[16,256,1024]{1,0,2:T(8,128)(2,1)} async-done(((bf16[16,256,1024]{1,0,2:T(8,128)(2,1)}), bf16[16,256,1024]{1,0,2:T(8,128)(2,1)}, u32[]{:S(2)}, u32[]{:S(2)}) %all-to-all-start.1) | async-done | bytes 8388640 | tf_op jit(solution)/shard_map/all_to_all | solution.py:47
  251.7 4.9 all-to-all-start.2
  256.7 9.4 %divide_convert_fusion.2 = bf16[16,256,1024]{2,1,0:T(8,128)(2,1)S(1)} fusion(f32[16,256,1024]{2,1,0:T(8,128)} %param.8, bf16[16,256,1024]{2,1,0:T(8,128)(2,1)} %param.9, f32[16,1024]{1,0:T(8,128)S(1)} %broadcast_multiply_fusion.2), kind=kLoop, calls=%fused_computation.6 | loop fusion | flops 16777216 | bytes 33619968 | tf_op jit(solution)/shard_map/convert_element_type | solution.py:41
  266.1 1.2 fusion.7
  268.6 1.2 fusion.5
  269.9 1.2 fusion.4
  271.1 1.2 fusion.3
  276.1 74.6 %all-to-all-done.2 = bf16[16,1024,256]{2,0,1:T(8,128)(2,1)} async-done(((bf16[16,1024,256]{2,0,1:T(8,128)(2,1)}), bf16[16,1024,256]{2,0,1:T(8,128)(2,1)}, u32[]{:S(2)}, u32[]{:S(2)}) %all-to-all-start.2) | async-done | bytes 8388640 | tf_op jit(solution)/shard_map/all_to_all | solution.py:49
  350.7 4.9 all-to-all-start
  355.7 97.2 %all_gather.6 = bf16[2048,16]{0,1:T(8,128)(2,1)S(1)} all-gather(bf16[256,16]{0,1:T(8,128)(2,1)S(1)} %multiply_convert_fusion), channel_id=1, replica_groups=mesh['bank'=4,'zero'=8] {'zero'}, dimensions={0}, use_global_device_ids=true | all-gather | bytes 73728 | tf_op jit(solution)/shard_map/all_gather | solution.py:60
  452.9 14.2 %all_gather.7 = bf16[2048,64]{0,1:T(8,128)(2,1)S(1)} all-gather(bf16[2048,16]{0,1:T(8,128)(2,1)S(1)} %all_gather.6), channel_id=1, replica_groups=mesh['bank'=4,'zero'=8] {'bank'}, dimensions={1}, use_global_device_ids=true | all-gather | bytes 327680 | tf_op jit(solution)/shard_map/all_gather | solution.py:61
  468.3 12.3 %copy.43 = bf16[16,8,256,128]{3,2,1,0:T(8,128)(2,1)} copy(bf16[16,8,256,128]{2,0,3,1:T(8,128)(2,1)} %bitcast.11) | data formatting | bytes 16777216 | tf_op jit(solution)/shard_map/all_to_all | solution.py:47
  480.6 11.4 %copy.48 = bf16[16,128,8,256]{3,2,1,0:T(8,128)(2,1)} copy(bf16[16,128,8,256]{3,0,1,2:T(8,128)(2,1)} %bitcast.14) | data formatting | bytes 16777216 | tf_op jit(solution)/shard_map/all_to_all | solution.py:49
  492.0 13.4 %all_to_all.37 = bf16[16,128,2048]{2,1,0:T(8,128)(2,1)} reshape(bf16[16,128,8,256]{3,2,1,0:T(8,128)(2,1)} %copy.48) | data formatting | bytes 16777216 | tf_op jit(solution)/shard_map/all_to_all | solution.py:49
  505.4 7.9 %copy.38 = bf16[16,8,256,128]{3,2,1,0:T(8,128)(2,1)} copy(bf16[16,8,256,128]{3,2,0,1:T(8,128)(2,1)} %bitcast.8) | data formatting | bytes 16777216 | tf_op jit(solution)/shard_map/reshape | solution.py:13
  (26 shorter events, 9.8 us)
Async XLA Ops:
  7.2 132.3 %all-reduce.3.cloned.1.call-start = ((), (), s32[]{:S(2)}) async-start(), calls=%async_computation.3 | async-start | bytes 393216 | tf_op jit(solution)/shard_map/psum | solution.py:29
  152.5 5.3 %copy-start.1 = (f32[16,1024]{1,0:T(8,128)S(1)}, f32[16,1024]{1,0:T(8,128)}, u32[]{:S(2)}) copy-start(f32[16,1024]{1,0:T(8,128)} %get-tuple-element.16) | copy-start | bytes 196612
  152.5 99.2 %all-to-all-start.1 = ((bf16[16,256,1024]{1,0,2:T(8,128)(2,1)}), bf16[16,256,1024]{1,0,2:T(8,128)(2,1)}, u32[]{:S(2)}, u32[]{:S(2)}) async-start(bf16[16,256,1024]{1,0,2:T(8,128)(2,1)} %divide_convert_fusion.1), calls=%async_computation.1 | async-start | bytes 16777216 | tf_op jit(solution)/shard_map/all_to_all | solution.py:47
  181.9 74.8 %copy-start = (f32[16,1024]{1,0:T(8,128)S(1)}, f32[16,1024]{1,0:T(8,128)}, u32[]{:S(2)}) copy-start(f32[16,1024]{1,0:T(8,128)} %get-tuple-element.14) | copy-start | bytes 196612
  251.7 99.0 %all-to-all-start.2 = ((bf16[16,1024,256]{2,0,1:T(8,128)(2,1)}), bf16[16,1024,256]{2,0,1:T(8,128)(2,1)}, u32[]{:S(2)}, u32[]{:S(2)}) async-start(bf16[16,1024,256]{2,0,1:T(8,128)(2,1)} %divide_convert_fusion), calls=%async_computation.2 | async-start | bytes 16777216 | tf_op jit(solution)/shard_map/all_to_all | solution.py:49
  276.1 79.6 %copy-start.2 = (f32[256,16]{0,1:T(8,128)S(1)}, f32[256,16]{0,1:T(8,128)}, u32[]{:S(2)}) copy-start(f32[256,16]{0,1:T(8,128)} %param.14) | copy-start | bytes 49156
  276.1 79.6 %copy-start.3 = (f32[256]{0:T(256)S(1)}, f32[256]{0:T(256)}, u32[]{:S(2)}) copy-start(f32[256]{0:T(256)} %param.15) | copy-start | bytes 3076
  350.7 154.7 %all-to-all-start = ((bf16[8,16,256,128]{3,2,1,0:T(8,128)(2,1)}), bf16[8,16,256,128]{3,2,1,0:T(8,128)(2,1)}, u32[]{:S(2)}, u32[]{:S(2)}) async-start(bf16[8,16,256,128]{3,2,1,0:T(8,128)(2,1)} %fusion), calls=%async_computation | async-start | bytes 16777216 | tf_op jit(solution)/shard_map/all_to_all | solution.py:12
Sparse Core Ops, SparseCore 0:
  82.4 57.0 all-reduce.2
